TPU v7x, 128 devices: a whole 4x4x4 slice. The times are simulated.
128 devices in a mesh: py: 4 (over y), pz: 32 (over z, x, core).
Axes of the slice: x: 4, y: 4, z: 4, core: 2. Of those that a mesh axis runs over, the one named last changes fastest.
Arguments:
- species: float32 [4, 512, 256, 256], P(None, None, 'py', 'pz'), may hold values from -6 to 6
- coupling: float32 [4, 4], replicated, may hold values from -4 to 4
- symbol_x: float32 [512], replicated, may hold values from 0.3 to 3
- symbol_y: float32 [256], replicated, may hold values from 0.3 to 3
- symbol_z: float32 [256], replicated, may hold values from 0.3 to 3
Outputs:
- modes: float32 [4, 512, 256, 256], P(None, 'py', 'pz')
All inputs are finite; a program needn't handle non-finite values.
Results may differ from a plain program's by a relative error of at most 0.00007.
Values sent between devices are 32-bit elements; how exact they have to be, the bound alone decides.
A program may use at most 64 MiB of HBM per device.

v0:
```python
import functools

import jax
import jax.numpy as jnp
import numpy as np
from jax import lax
from jax.experimental import pallas as pl
from jax.experimental.pallas import tpu as pltpu
from jax.sharding import PartitionSpec as P

MESH = pl.DeviceIdType.MESH
F32 = jnp.float32
BF16 = jnp.bfloat16


def mode_table(count):
    rank = 2 * np.arange(count, dtype=np.int64) + 1
    angle = (rank[:, None] * rank[None, :] % (8 * count)) * (np.pi / (4 * count))
    return (np.cos(angle) * np.sqrt(2.0 / count)).astype(np.float32)


def halves(table):
    high = table.astype(BF16)
    low = (table - high.astype(np.float32)).astype(BF16)
    return np.concatenate([high, low], axis=0)


def split(values):
    high = values.astype(BF16)
    low = (values - high.astype(F32)).astype(BF16)
    return high, low


def dot(lhs, rhs):
    return jnp.dot(lhs, rhs, preferred_element_type=F32)


def exchange_kernel(
    species_ref, hx_hbm, hy_hbm, hz_hbm, modes_ref,
    xin, hx, hy, hz, lhs_high, lhs_low, ysend, yrecv, p1send, p1recv, final,
    in_sem, table_sem, ys_sem, yr_sem, p1s_sem, p1r_sem, p2s_sem, p2r_sem,
):
    me_y = lax.axis_index("py")
    me_pz = lax.axis_index("pz")
    me_z = me_pz // 8
    me_x = (me_pz // 2) % 4
    me_c = me_pz % 2

    def at(z, x, c):
        return (me_y, z * 8 + x * 2 + c)

    def load_field(field):
        return [
            pltpu.make_async_copy(
                species_ref.at[field, :, :, pl.ds(128 * tile, 128)],
                xin.at[field, tile],
                in_sem.at[field, tile],
            )
            for tile in range(4)
        ]

    tables = [
        pltpu.make_async_copy(hx_hbm, hx, table_sem.at[0]),
        pltpu.make_async_copy(hy_hbm, hy, table_sem.at[1]),
        pltpu.make_async_copy(hz_hbm, hz, table_sem.at[2]),
    ]
    for copy in load_field(0):
        copy.start()
    tables[0].start()

    barrier = pltpu.get_barrier_semaphore()
    peers = [(lax.rem(me_y + d, 4), me_pz) for d in (1, 2, 3)]
    for d in (1, 2, 3):
        for c in (0, 1):
            peers.append(at(me_z, lax.rem(me_x + d, 4), c))
            peers.append(at(lax.rem(me_z + d, 4), me_x, c))
    peers.append(at(me_z, me_x, 1 - me_c))
    for peer in peers:
        pl.semaphore_signal(barrier, inc=1, device_id=peer, device_id_type=MESH)

    for field in (1, 2, 3):
        for copy in load_field(field):
            copy.start()
    tables[1].start()
    tables[2].start()
    tables[0].wait()

    def x_stage(field):
        for copy in load_field(field):
            copy.wait()
        for z in range(8):
            for tile in range(4):
                rows = xin.at[field, tile].reshape(512, 128)[pl.ds(z, 64, stride=8), :]
                high, low = split(rows)
                lhs_high[pl.ds(64 * z, 64), pl.ds(128 * tile, 128)] = high
                lhs_low[pl.ds(64 * z, 64), pl.ds(128 * tile, 128)] = low
        for half in range(2):
            high = lhs_high[pl.ds(256 * half, 256), :]
            low = lhs_low[pl.ds(256 * half, 256), :]
            for side in range(2):
                columns = pl.ds(256 * side, 256)
                table = hx[pl.ds(0, 512), columns]
                out = dot(high, table) + dot(low, table)
                out += dot(high, hx[pl.ds(512, 512), columns])
                for plane in range(4):
                    for part in range(2):
                        ysend[
                            field * 4 + half * 2 + plane // 2, side * 2 + part, plane % 2
                        ] = out[64 * plane : 64 * plane + 64, 128 * part : 128 * part + 128]

    def y_send(piece):
        for d in (1, 3, 2):
            to = lax.rem(me_y + d, 4)
            pltpu.make_async_remote_copy(
                src_ref=ysend.at[piece, to],
                dst_ref=yrecv.at[piece, :, me_y],
                send_sem=ys_sem.at[piece],
                recv_sem=yr_sem.at[piece],
                device_id=(to, me_pz),
                device_id_type=MESH,
            ).start()
        yrecv[piece, :, me_y] = ysend[piece, me_y]

    x_stage(0)
    pl.semaphore_wait(barrier, len(peers))
    for piece in range(4):
        y_send(piece)

    @pl.loop(1, 4)
    def _(field):
        x_stage(field)
        for pair in range(4):
            y_send(field * 4 + pair)

    tables[1].wait()
    tables[2].wait()

    def y_stage(piece):
        all_y = yrecv.at[piece, :, pl.ds(0, 3)]
        pltpu.make_async_copy(all_y, all_y, yr_sem.at[piece]).wait()
        data = jnp.concatenate(
            [yrecv[piece, plane].reshape(256, 128) for plane in range(2)], axis=1
        )
        high, low = split(data)
        out = dot(hy[pl.ds(0, 256), :], high) + dot(hy[pl.ds(256, 256), :], high)
        out += dot(hy[pl.ds(0, 256), :], low)
        for plane in range(2):
            p1send[piece, :, :, :, plane] = out[:, 128 * plane : 128 * plane + 128].reshape(
                4, 4, 2, 8, 128
            )

    def first_send(piece, along_x):
        for d in (1, 3, 2):
            if along_x:
                to = lax.rem(me_x + d, 4)
                src, device = p1send.at[piece, :, to], at(me_z, to, me_c)
                dst = p1recv.at[piece, me_x]
            else:
                to = lax.rem(me_z + d, 4)
                src, device = p1send.at[piece, to], at(to, me_x, me_c)
                dst = p1recv.at[piece, me_z]
            pltpu.make_async_remote_copy(
                src_ref=src, dst_ref=dst,
                send_sem=p1s_sem.at[piece], recv_sem=p1r_sem.at[piece],
                device_id=device, device_id_type=MESH,
            ).start()
        if along_x:
            p1recv[piece, me_x] = p1send[piece, :, me_x]
        else:
            p1recv[piece, me_z] = p1send[piece, me_z]

    def second_send(piece, along_x):
        arrived = p1recv.at[piece, pl.ds(0, 3)]
        pltpu.make_async_copy(arrived, arrived, p1r_sem.at[piece]).wait()
        for d in (1, 3, 2, 0):
            for c in (me_c, 1 - me_c):
                if along_x:
                    to = lax.rem(me_x + d, 4)
                    device, dst = at(me_z, to, c), final.at[piece, :, me_x, me_c]
                else:
                    to = lax.rem(me_z + d, 4)
                    device, dst = at(to, me_x, c), final.at[piece, me_z, :, me_c]
                if d == 0 and c is me_c:
                    continue
                pltpu.make_async_remote_copy(
                    src_ref=p1recv.at[piece, :, to, c], dst_ref=dst,
                    send_sem=p2s_sem.at[piece], recv_sem=p2r_sem.at[piece],
                    device_id=device, device_id_type=MESH,
                ).start()
        if along_x:
            final[piece, :, me_x, me_c] = p1recv[piece, :, me_x, me_c]
        else:
            final[piece, me_z, :, me_c] = p1recv[piece, :, me_z, me_c]

    def z_stage(field):
        for pair in range(4):
            arrived = final.at[field * 4 + pair].reshape(512, 128).at[pl.ds(0, 448)]
            pltpu.make_async_copy(arrived, arrived, p2r_sem.at[field * 4 + pair]).wait()
        for ky in range(8):
            data = jnp.concatenate(
                [
                    final.at[field * 4 + pair].reshape(512, 128)[pl.ds(ky, 64, stride=8), :]
                    for pair in range(4)
                ],
                axis=0,
            )
            high, low = split(data.T)
            table = hz[pl.ds(0, 256), :]
            out = dot(high, table) + dot(low, table) + dot(high, hz[pl.ds(256, 256), :])
            for part in range(2):
                modes_ref.at[field, part].reshape(1024, 128)[pl.ds(ky, 128, stride=8), :] = out[
                    :, 128 * part : 128 * part + 128
                ]

    def second_pair(step):
        second_send(2 * step, False)
        second_send(2 * step + 1, True)

    @pl.loop(0, 4)
    def _(field):
        for half in range(2):
            step = 2 * field + half
            if half == 0:
                @pl.when(field > 0)
                def _():
                    second_pair(step - 1)
            else:
                second_pair(step - 1)
            y_stage(2 * step)
            first_send(2 * step, True)
            y_stage(2 * step + 1)
            first_send(2 * step + 1, False)
            if half == 0:
                @pl.when(field >= 2)
                def _():
                    z_stage(field - 2)

    second_pair(7)
    z_stage(2)
    z_stage(3)

    @pl.loop(0, 16)
    def _(piece):
        sent = ysend.at[piece, pl.ds(0, 3)]
        pltpu.make_async_copy(sent, sent, ys_sem.at[piece]).wait()
        sent = p1recv.at[piece, pl.ds(0, 3)]
        pltpu.make_async_copy(sent, sent, p1s_sem.at[piece]).wait()
        sent = final.at[piece].reshape(512, 128).at[pl.ds(0, 448)]
        pltpu.make_async_copy(sent, sent, p2s_sem.at[piece]).wait()


def exchange(species, hx, hy, hz):
    dma = pltpu.SemaphoreType.DMA
    anywhere = pl.BlockSpec(memory_space=pl.ANY)
    return pl.pallas_call(
        exchange_kernel,
        out_shape=jax.ShapeDtypeStruct((4, 2, 128, 8, 128), F32),
        in_specs=[anywhere] * 4,
        out_specs=pl.BlockSpec(memory_space=pltpu.VMEM),
        scratch_shapes=[
            pltpu.VMEM((4, 4, 64, 8, 128), F32),
            pltpu.VMEM((1024, 512), BF16),
            pltpu.VMEM((512, 256), BF16),
            pltpu.VMEM((512, 256), BF16),
            pltpu.VMEM((512, 512), BF16),
            pltpu.VMEM((512, 512), BF16),
            pltpu.VMEM((16, 4, 2, 64, 128), F32),
            pltpu.VMEM((16, 2, 4, 64, 128), F32),
            pltpu.VMEM((16, 4, 4, 2, 2, 8, 128), F32),
            pltpu.VMEM((16, 4, 4, 2, 2, 8, 128), F32),
            pltpu.VMEM((16, 4, 4, 2, 2, 8, 128), F32),
            dma((4, 4)),
            dma((3,)),
            dma((16,)),
            dma((16,)),
            dma((16,)),
            dma((16,)),
            dma((16,)),
            dma((16,)),
        ],
        compiler_params=pltpu.CompilerParams(
            collective_id=0, has_side_effects=True, vmem_limit_bytes=40 * 2**20
        ),
        name="exchange",
    )(species, hx, hy, hz)


def mix_kernel(modes_ref, coupling_ref, symbol_x_ref, symbol_yz_ref, out_ref):
    block = out_ref.shape[1]
    first = pl.program_id(0) * block

    @pl.loop(0, block)
    def _(row):
        for part in range(2):
            lanes = pl.ds(128 * part, 128)
            weight = 1.0 / (symbol_x_ref[first + row] + symbol_yz_ref[:, lanes])
            old = [modes_ref[a, part, row] for a in range(4)]
            for a in range(4):
                mixed = coupling_ref[a, 0] * old[0]
                for b in range(1, 4):
                    mixed += coupling_ref[a, b] * old[b]
                out_ref[a, row, :, lanes] = mixed + weight * (old[a] - mixed)


def mix(modes, coupling, part_x, symbol_yz):
    steps = 8
    block = 128 // steps
    smem = pl.BlockSpec(memory_space=pltpu.SMEM)
    return pl.pallas_call(
        mix_kernel,
        grid=(steps,),
        out_shape=jax.ShapeDtypeStruct((4, 128, 8, 256), F32),
        in_specs=[
            pl.BlockSpec((4, 2, block, 8, 128), lambda i: (0, 0, i, 0, 0)),
            smem,
            smem,
            pl.BlockSpec((8, 256), lambda i: (0, 0)),
        ],
        out_specs=pl.BlockSpec((4, block, 8, 256), lambda i: (0, i, 0, 0)),
        name="mix",
    )(modes, coupling, part_x, symbol_yz)


def shards(species, coupling, symbol_x, symbol_y, symbol_z):
    hx = halves(mode_table(512))
    hy = halves(mode_table(256))
    table_z = mode_table(256).reshape(32, 4, 2, 256).transpose(1, 0, 2, 3).reshape(256, 256)
    hz = halves(table_z)
    modes = exchange(species.transpose(0, 2, 3, 1), hx, hy, hz)
    part_x = lax.dynamic_slice_in_dim(symbol_x, lax.axis_index("py") * 128, 128)
    part_y = lax.dynamic_slice_in_dim(symbol_y, lax.axis_index("pz") * 8, 8)
    symbol_yz = 1.0 + part_y[:, None] + symbol_z[None, :]
    return mix(modes, coupling, part_x, symbol_yz)


def solution(mesh):
    return jax.shard_map(
        shards,
        mesh=mesh,
        in_specs=(P(None, None, "py", "pz"), P(), P(), P(), P()),
        out_specs=P(None, "py", "pz", None),
        check_vma=False,
    )
```

profile of v0, /device:TPU:1, one launch (start us, length us, event | category | flops | bytes accessed | tf_op | source)
XLA Modules:
  0.0 102.2 jit_solution(7027519054598714006)
XLA Ops:
  0.0 0.8 dynamic-slice_add_fusion
  0.8 1.3 %dynamic_slice.6.symbol_x_ref = f32[128]{0:T(128)} dynamic-slice(f32[512]{0:T(512)} %param.10, s32[]{:T(128)S(6)} %select_n.6), dynamic_slice_sizes={128} | dynamic-slice | bytes 1028 | tf_op jit(solution)/shard_map/dynamic_slice | solution.py:330
  2.0 1.3 %broadcast_add_fusion.symbol_yz_ref = f32[8,256]{1,0:T(8,128)} fusion(f32[256]{0:T(256)} %param.12, f32[8]{0:T(128)S(1)} %dynamic-slice_add_fusion), kind=kLoop, calls=%fused_computation | loop fusion | flops 2048 | bytes 9248 | tf_op jit(solution)/shard_map/add | solution.py:332
  3.4 0.0 copy-start.1
  3.4 2.2 %copy-done.1 = f32[4,512,64,8]{1,3,2,0:T(8,128)S(1)} copy-done((f32[4,512,64,8]{1,3,2,0:T(8,128)S(1)}, f32[4,512,64,8]{1,3,2,0:T(8,128)}, u32[]{:S(2)}) %copy-start.1) | copy-done | bytes 4194328
  5.6 0.0 copy-start.2
  5.6 1.2 %copy-done.2 = bf16[1024,512]{1,0:T(8,128)(2,1)S(1)} copy-done((bf16[1024,512]{1,0:T(8,128)(2,1)S(1)}, bf16[1024,512]{1,0:T(8,128)(2,1)}, u32[]{:S(2)}) %copy-start.2) | copy-done | bytes 1048600
  6.8 0.0 copy-start.3
  6.8 0.9 copy-done.3
  7.8 0.0 copy-start.4
  7.8 0.9 copy-done.4
  8.7 83.8 %exchange.1.modes_ref = f32[4,2,128,8,128]{4,3,2,1,0:T(8,128)S(1)} custom-call(f32[4,64,8,512]{3,2,1,0:T(8,128)S(1)} %bitcast.1, bf16[1024,512]{1,0:T(8,128)(2,1)S(1)} %copy-done.2, bf16[512,256]{1,0:T(8,128)(2,1)S(1)} %copy-done.4, bf16[512,256]{1,0:T(8,128)(2,1)S(1)} %copy-done.3), custom_call_target="tpu_custom_call" | custom-call | tf_op jit(solution)/shard_map/exchange/pallas_call | solution.py:255
  92.5 0.0 copy-start
  92.5 1.9 %copy-done = f32[4,2,128,8,128]{4,3,2,1,0:T(8,128)} copy-done((f32[4,2,128,8,128]{4,3,2,1,0:T(8,128)}, f32[4,2,128,8,128]{4,3,2,1,0:T(8,128)S(1)}, u32[]{:S(2)}) %copy-start) | copy-done | bytes 4194328
  94.4 7.8 %mix.1 = f32[4,128,8,256]{3,2,1,0:T(8,128)} custom-call(f32[4,2,128,8,128]{4,3,2,1,0:T(8,128)} %copy-done, f32[4,4]{1,0:T(4,128)} %coupling_ref.1, f32[128]{0:T(128)} %dynamic_slice.6.symbol_x_ref, f32[8,256]{1,0:T(8,128)} %broadcast_add_fusion.symbol_yz_ref), custom_call_target="tpu_custom_call" | custom-call | tf_op jit(solution)/shard_map/mix/pallas_call | solution.py:309
Async XLA Ops:
  3.4 2.2 %copy-start.1 = (f32[4,512,64,8]{1,3,2,0:T(8,128)S(1)}, f32[4,512,64,8]{1,3,2,0:T(8,128)}, u32[]{:S(2)}) copy-start(f32[4,512,64,8]{1,3,2,0:T(8,128)} %param.8) | copy-start | bytes 12582916
  5.6 1.2 %copy-start.2 = (bf16[1024,512]{1,0:T(8,128)(2,1)S(1)}, bf16[1024,512]{1,0:T(8,128)(2,1)}, u32[]{:S(2)}) copy-start(bf16[1024,512]{1,0:T(8,128)(2,1)} %constant.27.clone.hx_hbm) | copy-start | bytes 3145732
  6.8 0.9 copy-start.3
  7.8 0.9 copy-start.4
  92.5 1.9 %copy-start = (f32[4,2,128,8,128]{4,3,2,1,0:T(8,128)}, f32[4,2,128,8,128]{4,3,2,1,0:T(8,128)S(1)}, u32[]{:S(2)}) copy-start(f32[4,2,128,8,128]{4,3,2,1,0:T(8,128)S(1)} %exchange.1.modes_ref) | copy-start | bytes 12582916
where the time goes:
time: 103 us; the launch traced here: 102 us
  Pallas kernels  91.6 us (89%)
  local copies, waits for them, and re-layouts  8.53 us (8%)
  other arithmetic  2.09 us (2%)
    pallas_call x1, Pallas kernels, exchange(): pl.pallas_call(exchange_kernel, out_shape=jax.ShapeDtypeStruct((4, 2, 128...  83.8 us
    pallas_call x1, Pallas kernels, mix(): pl.pallas_call(mix_kernel, grid=(steps,), out_shape=jax.ShapeDtypeStruct(...  7.8 us
    unnamed x10, local copies, waits for them, and re-layouts  7.24 us
    add x2, other arithmetic, shards(): symbol_yz = 1.0 + part_y[:, None] + symbol_z[None, :]  2.09 us

commit v1 on v0

v1 whole, which is shorter than its diff:
```python
import functools

import jax
import jax.numpy as jnp
import numpy as np
from jax import lax
from jax.experimental import pallas as pl
from jax.experimental.pallas import tpu as pltpu
from jax.sharding import PartitionSpec as P

MESH = pl.DeviceIdType.MESH
F32 = jnp.float32
BF16 = jnp.bfloat16
AHEAD = 3
LAG = 2


def mode_table(count):
    rank = 2 * np.arange(count, dtype=np.int64) + 1
    angle = (rank[:, None] * rank[None, :] % (8 * count)) * (np.pi / (4 * count))
    return (np.cos(angle) * np.sqrt(2.0 / count)).astype(np.float32)


def halves(table):
    high = table.astype(BF16)
    low = (table - high.astype(np.float32)).astype(BF16)
    return np.concatenate([high, low], axis=0)


def split(values):
    high = values.astype(BF16)
    low = (values - high.astype(F32)).astype(BF16)
    return high, low


def dot(lhs, rhs):
    return jnp.dot(lhs, rhs, preferred_element_type=F32)


def exchange_kernel(
    species_ref, table, modes_ref,
    xin, lhs_high, lhs_low, ysend, yrecv, p1send, p1recv, final,
    in_sem, ys_sem, yr_sem, p1s_sem, p1r_sem, p2s_sem, p2r_sem,
):
    me_y = lax.axis_index("py")
    me_pz = lax.axis_index("pz")
    me_z = me_pz // 8
    me_x = (me_pz // 2) % 4
    me_c = me_pz % 2

    def at(z, x, c):
        return (me_y, z * 8 + x * 2 + c)

    def load_field(field):
        return [
            pltpu.make_async_copy(
                species_ref.at[field, :, :, pl.ds(128 * tile, 128)],
                xin.at[field, tile],
                in_sem.at[field, tile],
            )
            for tile in range(4)
        ]

    y_high = table.at[pl.ds(1024, 256), pl.ds(0, 256)]
    y_low = table.at[pl.ds(1280, 256), pl.ds(0, 256)]
    z_high = table.at[pl.ds(1024, 256), pl.ds(256, 256)]
    z_low = table.at[pl.ds(1280, 256), pl.ds(256, 256)]

    for copy in load_field(0):
        copy.start()

    barrier = pltpu.get_barrier_semaphore()
    peers = [(lax.rem(me_y + d, 4), me_pz) for d in (1, 2, 3)]
    for d in (1, 2, 3):
        for c in (0, 1):
            peers.append(at(me_z, lax.rem(me_x + d, 4), c))
            peers.append(at(lax.rem(me_z + d, 4), me_x, c))
    peers.append(at(me_z, me_x, 1 - me_c))
    for peer in peers:
        pl.semaphore_signal(barrier, inc=1, device_id=peer, device_id_type=MESH)

    for field in (1, 2, 3):
        for copy in load_field(field):
            copy.start()

    def x_stage(field, half):
        for plane in range(4):
            for tile in range(4):
                rows = xin.at[field, tile].reshape(512, 128)[
                    pl.ds(4 * half + plane, 64, stride=8), :
                ]
                high, low = split(rows)
                lhs_high[pl.ds(64 * plane, 64), pl.ds(128 * tile, 128)] = high
                lhs_low[pl.ds(64 * plane, 64), pl.ds(128 * tile, 128)] = low
        for side in range(2):
            columns = pl.ds(256 * side, 256)
            x_high = table[pl.ds(0, 512), columns]
            out = dot(lhs_high[...], x_high) + dot(lhs_low[...], x_high)
            out += dot(lhs_high[...], table[pl.ds(512, 512), columns])
            for plane in range(4):
                for part in range(2):
                    ysend[
                        field * 4 + half * 2 + plane // 2, side * 2 + part, plane % 2
                    ] = out[64 * plane : 64 * plane + 64, 128 * part : 128 * part + 128]

    def y_send(piece):
        for d in (1, 3, 2):
            to = lax.rem(me_y + d, 4)
            pltpu.make_async_remote_copy(
                src_ref=ysend.at[piece, to],
                dst_ref=yrecv.at[piece, :, me_y],
                send_sem=ys_sem.at[piece],
                recv_sem=yr_sem.at[piece],
                device_id=(to, me_pz),
                device_id_type=MESH,
            ).start()
        yrecv[piece, :, me_y] = ysend[piece, me_y]

    def y_stage(piece):
        all_y = yrecv.at[piece, :, pl.ds(0, 3)]
        pltpu.make_async_copy(all_y, all_y, yr_sem.at[piece]).wait()
        data = jnp.concatenate(
            [yrecv[piece, plane].reshape(256, 128) for plane in range(2)], axis=1
        )
        high, low = split(data)
        out = dot(y_high[...], high) + dot(y_low[...], high) + dot(y_high[...], low)
        for plane in range(2):
            p1send[piece, plane] = out[:, 128 * plane : 128 * plane + 128].reshape(
                4, 4, 2, 8, 128
            )

    def first_send(piece):
        for d in (1, 3, 2):
            for plane in range(2):
                if plane == 0:
                    to = lax.rem(me_x + d, 4)
                    src, device = p1send.at[piece, 0, :, to], at(me_z, to, me_c)
                    dst = p1recv.at[piece, 0, me_x]
                else:
                    to = lax.rem(me_z + d, 4)
                    src, device = p1send.at[piece, 1, to], at(to, me_x, me_c)
                    dst = p1recv.at[piece, 1, me_z]
                pltpu.make_async_remote_copy(
                    src_ref=src, dst_ref=dst,
                    send_sem=p1s_sem.at[piece], recv_sem=p1r_sem.at[piece, plane],
                    device_id=device, device_id_type=MESH,
                ).start()
        p1recv[piece, 0, me_x] = p1send[piece, 0, :, me_x]
        p1recv[piece, 1, me_z] = p1send[piece, 1, me_z]

    def second_send(piece):
        for plane in range(2):
            arrived = p1recv.at[piece, plane, pl.ds(0, 3)]
            pltpu.make_async_copy(arrived, arrived, p1r_sem.at[piece, plane]).wait()
            for d in (1, 3, 2, 0):
                for c in (me_c, 1 - me_c):
                    if d == 0 and c is me_c:
                        continue
                    if plane == 0:
                        to = lax.rem(me_z + d, 4)
                        device, dst = at(to, me_x, c), final.at[piece, 0, me_z, :, me_c]
                    else:
                        to = lax.rem(me_x + d, 4)
                        device, dst = at(me_z, to, c), final.at[piece, 1, :, me_x, me_c]
                    pltpu.make_async_remote_copy(
                        src_ref=p1recv.at[piece, plane, :, to, c], dst_ref=dst,
                        send_sem=p2s_sem.at[piece], recv_sem=p2r_sem.at[piece],
                        device_id=device, device_id_type=MESH,
                    ).start()
        final[piece, 0, me_z, :, me_c] = p1recv[piece, 0, :, me_z, me_c]
        final[piece, 1, :, me_x, me_c] = p1recv[piece, 1, :, me_x, me_c]

    def seven_eighths(piece):
        return final.at[piece].reshape(512, 128).at[pl.ds(0, 448)]

    def z_stage(field):
        for pair in range(4):
            arrived = seven_eighths(field * 4 + pair)
            pltpu.make_async_copy(arrived, arrived, p2r_sem.at[field * 4 + pair]).wait()
        for ky in range(8):
            data = jnp.concatenate(
                [
                    final.at[field * 4 + pair, plane].reshape(256, 128)[
                        pl.ds(ky, 32, stride=8), :
                    ]
                    for pair in range(4)
                    for plane in range(2)
                ],
                axis=0,
            )
            high, low = split(data.T)
            out = dot(high, z_high[...]) + dot(low, z_high[...]) + dot(high, z_low[...])
            for part in range(2):
                modes_ref.at[field, part].reshape(1024, 128)[pl.ds(ky, 128, stride=8), :] = out[
                    :, 128 * part : 128 * part + 128
                ]

    for group in range(AHEAD):
        if group % 2 == 0:
            for copy in load_field(group // 2):
                copy.wait()
        x_stage(group // 2, group % 2)
        if group == 0:
            pl.semaphore_wait(barrier, len(peers))
        y_send(2 * group)
        y_send(2 * group + 1)

    @pl.loop(0, 8)
    def _(step):
        for part in range(2):
            piece = 2 * step + part
            y_stage(piece)
            first_send(piece)

            if part == 0:
                group = step + AHEAD

                @pl.when((group < 8) & (group % 2 == 0))
                def _():
                    for copy in load_field(group // 2):
                        copy.wait()

                @pl.when(group < 8)
                def _():
                    x_stage(group // 2, group % 2)
                    y_send(2 * group)
                    y_send(2 * group + 1)

            @pl.when(piece >= LAG)
            def _():
                second_send(piece - LAG)

        @pl.when((step == 4) | (step == 6))
        def _():
            z_stage((step - 4) // 2)

    for piece in range(16 - LAG, 16):
        second_send(piece)
    z_stage(2)
    z_stage(3)

    @pl.loop(0, 16)
    def _(piece):
        sent = ysend.at[piece, pl.ds(0, 3)]
        pltpu.make_async_copy(sent, sent, ys_sem.at[piece]).wait()
        sent = p1recv.at[piece, :, pl.ds(0, 3)]
        pltpu.make_async_copy(sent, sent, p1s_sem.at[piece]).wait()
        sent = seven_eighths(piece)
        pltpu.make_async_copy(sent, sent, p2s_sem.at[piece]).wait()


def exchange(species, table):
    dma = pltpu.SemaphoreType.DMA
    return pl.pallas_call(
        exchange_kernel,
        out_shape=jax.ShapeDtypeStruct((4, 2, 128, 8, 128), F32),
        in_specs=[
            pl.BlockSpec(memory_space=pl.ANY),
            pl.BlockSpec(memory_space=pltpu.VMEM),
        ],
        out_specs=pl.BlockSpec(memory_space=pltpu.VMEM),
        scratch_shapes=[
            pltpu.VMEM((4, 4, 64, 8, 128), F32),
            pltpu.VMEM((256, 512), BF16),
            pltpu.VMEM((256, 512), BF16),
            pltpu.VMEM((16, 4, 2, 64, 128), F32),
            pltpu.VMEM((16, 2, 4, 64, 128), F32),
            pltpu.VMEM((16, 2, 4, 4, 2, 8, 128), F32),
            pltpu.VMEM((16, 2, 4, 4, 2, 8, 128), F32),
            pltpu.VMEM((16, 2, 4, 4, 2, 8, 128), F32),
            dma((4, 4)),
            dma((16,)),
            dma((16,)),
            dma((16,)),
            dma((16, 2)),
            dma((16,)),
            dma((16,)),
        ],
        compiler_params=pltpu.CompilerParams(
            collective_id=0, has_side_effects=True, vmem_limit_bytes=48 * 2**20
        ),
        name="exchange",
    )(species, table)


def mix_kernel(modes_ref, coupling_ref, symbol_x_ref, symbol_y_ref, symbol_z_ref, out_ref):
    block = out_ref.shape[1]
    first = pl.program_id(0) * block
    first_x = lax.axis_index("py") * 128 + first
    first_y = lax.axis_index("pz") * 8
    row_y = lax.broadcasted_iota(jnp.int32, (8, 256), 0)
    symbol_yz = 1.0 + jnp.broadcast_to(symbol_z_ref[...], (8, 256))
    part_y = jnp.zeros((8, 256), F32)
    for k in range(8):
        part_y = jnp.where(row_y == k, symbol_y_ref[first_y + k], part_y)
    symbol_yz = symbol_yz + part_y

    for row in range(block):
        for part in range(2):
            lanes = slice(128 * part, 128 * part + 128)
            weight = 1.0 / (symbol_x_ref[first_x + row] + symbol_yz[:, lanes])
            old = [modes_ref[a, part, first + row] for a in range(4)]
            for a in range(4):
                mixed = coupling_ref[a, 0] * old[0]
                for b in range(1, 4):
                    mixed += coupling_ref[a, b] * old[b]
                out_ref[a, row, :, lanes] = mixed + weight * (old[a] - mixed)


def mix(modes, coupling, symbol_x, symbol_y, symbol_z):
    steps = 8
    block = 128 // steps
    smem = pl.BlockSpec(memory_space=pltpu.SMEM)
    return pl.pallas_call(
        mix_kernel,
        grid=(steps,),
        out_shape=jax.ShapeDtypeStruct((4, 128, 8, 256), F32),
        in_specs=[
            pl.BlockSpec(memory_space=pltpu.VMEM),
            smem,
            smem,
            smem,
            pl.BlockSpec(memory_space=pltpu.VMEM),
        ],
        out_specs=pl.BlockSpec((4, block, 8, 256), lambda i: (0, i, 0, 0)),
        compiler_params=pltpu.CompilerParams(vmem_limit_bytes=12 * 2**20),
        name="mix",
    )(modes, coupling, symbol_x, symbol_y, symbol_z.reshape(1, 256))


def shards(species, coupling, symbol_x, symbol_y, symbol_z):
    table_z = mode_table(256).reshape(32, 8, 256).transpose(1, 0, 2).reshape(256, 256)
    tables_yz = np.concatenate([halves(mode_table(256)), halves(table_z)], axis=1)
    table = np.concatenate([halves(mode_table(512)), tables_yz], axis=0)
    modes = exchange(species.transpose(0, 2, 3, 1), table)
    return mix(modes, coupling, symbol_x, symbol_y, symbol_z)


def solution(mesh):
    return jax.shard_map(
        shards,
        mesh=mesh,
        in_specs=(P(None, None, "py", "pz"), P(), P(), P(), P()),
        out_specs=P(None, "py", "pz", None),
        check_vma=False,
    )
```

time: 103 us -> 73.1 us (0.71)
  Pallas kernels: 91.6 us -> 71.5 us
  local copies, waits for them, and re-layouts: 8.53 us -> 1.42 us
  other arithmetic: 2.09 us -> 0 us
    pallas_call x1, Pallas kernels: 83.8 us -> 66.6 us  [exchange(): pl.pallas_call(exchange_kernel, out_shape=jax.ShapeDtypeStruct((4, 2, 128...]
    unnamed x10, local copies, waits for them, and re-layouts: 7.24 us -> 1.42 us
    pallas_call x1, Pallas kernels: 7.8 us -> 4.9 us  [mix(): pl.pallas_call(mix_kernel, grid=(steps,), out_shape=jax.ShapeDtypeStruct(...]
    add x2 -> x0, other arithmetic: 2.09 us -> none  [shards(): symbol_yz = 1.0 + part_y[:, None] + symbol_z[None, :]]
    dynamic_slice x1 -> x0, local copies, waits for them, and re-layouts: 1.29 us -> none  [shards(): part_x = lax.dynamic_slice_in_dim(symbol_x, lax.axis_index('py') * 128, 128)]
where the time goes in v1:
time: 73.1 us; the launch traced here: 72.9 us
  Pallas kernels  71.5 us (98%)
  local copies, waits for them, and re-layouts  1.42 us (2%)
    pallas_call x1, Pallas kernels, exchange(): pl.pallas_call(exchange_kernel, out_shape=jax.ShapeDtypeStruct((4, 2, 128...  66.6 us
    pallas_call x1, Pallas kernels, mix(): pl.pallas_call(mix_kernel, grid=(steps,), out_shape=jax.ShapeDtypeStruct(...  4.9 us

profile of v1, /device:TPU:1, one launch (start us, length us, event | category | flops | bytes accessed | tf_op | source)
XLA Modules:
  0.0 72.9 jit_solution(13108861372588965158)
XLA Ops:
  0.0 0.0 copy-start
  0.0 1.4 %copy-done = bf16[1536,512]{1,0:T(8,128)(2,1)S(1)} copy-done((bf16[1536,512]{1,0:T(8,128)(2,1)S(1)}, bf16[1536,512]{1,0:T(8,128)(2,1)}, u32[]{:S(2)}) %copy-start) | copy-done | bytes 1572888
  1.4 0.0 copy-start.1
  1.4 0.0 copy-start.2
  1.4 0.0 copy-start.3
  1.4 0.0 copy-start.4
  1.4 66.6 %exchange.1.modes_ref = f32[4,2,128,8,128]{4,3,2,1,0:T(8,128)S(1)} custom-call(f32[4,64,8,512]{3,2,1,0:T(8,128)} %bitcast.3, bf16[1536,512]{1,0:T(8,128)(2,1)S(1)} %copy-done), custom_call_target="tpu_custom_call" | custom-call | tf_op jit(solution)/shard_map/exchange/pallas_call | solution.py:254
  68.0 0.0 copy-done.1
  68.0 0.0 copy-done.2
  68.0 0.0 copy-done.3
  68.0 0.0 copy-done.4
  68.0 4.9 %mix.1 = f32[4,128,8,256]{3,2,1,0:T(8,128)} custom-call(f32[4,2,128,8,128]{4,3,2,1,0:T(8,128)S(1)} %exchange.1.modes_ref, f32[4,4]{1,0:T(4,128)S(1)} %copy-done.1, f32[512]{0:T(512)S(1)} %copy-done.2, f32[256]{0:T(256)S(1)} %copy-done.3, f32[1,256]{1,0:T(1,128)S(1)} %bitcast.2), custom_call_target="tpu_custom_call" | custom-call | tf_op jit(solution)/shard_map/mix/pallas_call | solution.py:314
Async XLA Ops:
  0.0 1.4 %copy-start = (bf16[1536,512]{1,0:T(8,128)(2,1)S(1)}, bf16[1536,512]{1,0:T(8,128)(2,1)}, u32[]{:S(2)}) copy-start(bf16[1536,512]{1,0:T(8,128)(2,1)} %constant.2.clone.table) | copy-start | bytes 4718596
  1.4 66.6 %copy-start.1 = (f32[4,4]{1,0:T(4,128)S(1)}, f32[4,4]{1,0:T(4,128)}, u32[]{:S(2)}) copy-start(f32[4,4]{1,0:T(4,128)} %coupling_ref.1) | copy-start | bytes 196
  1.4 66.6 %copy-start.2 = (f32[512]{0:T(512)S(1)}, f32[512]{0:T(512)}, u32[]{:S(2)}) copy-start(f32[512]{0:T(512)} %symbol_x_ref.1) | copy-start | bytes 6148
  1.4 66.6 %copy-start.3 = (f32[256]{0:T(256)S(1)}, f32[256]{0:T(256)}, u32[]{:S(2)}) copy-start(f32[256]{0:T(256)} %symbol_y_ref.1) | copy-start | bytes 3076
  1.4 66.6 %copy-start.4 = (f32[256]{0:T(256)S(1)}, f32[256]{0:T(256)}, u32[]{:S(2)}) copy-start(f32[256]{0:T(256)} %param.10) | copy-start | bytes 3076

commit v2 on v1

--- a/solution.py
+++ b/solution.py
@@ -13,6 +13,7 @@
 BF16 = jnp.bfloat16
 AHEAD = 3
 LAG = 2
+MIX_STEPS = 8
 
 
 def mode_table(count):
@@ -38,9 +39,9 @@
 
 
 def exchange_kernel(
-    species_ref, table, modes_ref,
-    xin, lhs_high, lhs_low, ysend, yrecv, p1send, p1recv, final,
-    in_sem, ys_sem, yr_sem, p1s_sem, p1r_sem, p2s_sem, p2r_sem,
+    species_ref, table_hbm, modes_ref,
+    xin, table, lhs_high, lhs_low, ysend, yrecv, p1send, p1recv, final,
+    in_sem, table_sem, ys_sem, yr_sem, p1s_sem, p1r_sem, p2s_sem, p2r_sem,
 ):
     me_y = lax.axis_index("py")
     me_pz = lax.axis_index("pz")
@@ -66,8 +67,13 @@
     z_high = table.at[pl.ds(1024, 256), pl.ds(256, 256)]
     z_low = table.at[pl.ds(1280, 256), pl.ds(256, 256)]
 
+    tables = [
+        pltpu.make_async_copy(table_hbm.at[rows], table.at[rows], table_sem.at[k])
+        for k, rows in enumerate((pl.ds(0, 1024), pl.ds(1024, 512)))
+    ]
     for copy in load_field(0):
         copy.start()
+    tables[0].start()
 
     barrier = pltpu.get_barrier_semaphore()
     peers = [(lax.rem(me_y + d, 4), me_pz) for d in (1, 2, 3)]
@@ -82,6 +88,7 @@
     for field in (1, 2, 3):
         for copy in load_field(field):
             copy.start()
+    tables[1].start()
 
     def x_stage(field, half):
         for plane in range(4):
@@ -195,6 +202,7 @@
                     :, 128 * part : 128 * part + 128
                 ]
 
+    tables[0].wait()
     for group in range(AHEAD):
         if group % 2 == 0:
             for copy in load_field(group // 2):
@@ -205,6 +213,8 @@
         y_send(2 * group)
         y_send(2 * group + 1)
 
+    tables[1].wait()
+
     @pl.loop(0, 8)
     def _(step):
         for part in range(2):
@@ -253,14 +263,15 @@
     dma = pltpu.SemaphoreType.DMA
     return pl.pallas_call(
         exchange_kernel,
-        out_shape=jax.ShapeDtypeStruct((4, 2, 128, 8, 128), F32),
+        out_shape=pltpu.VMEM((4, 2, 128, 8, 128), F32),
         in_specs=[
             pl.BlockSpec(memory_space=pl.ANY),
-            pl.BlockSpec(memory_space=pltpu.VMEM),
+            pl.BlockSpec(memory_space=pl.ANY),
         ],
         out_specs=pl.BlockSpec(memory_space=pltpu.VMEM),
         scratch_shapes=[
             pltpu.VMEM((4, 4, 64, 8, 128), F32),
+            pltpu.VMEM((1536, 512), BF16),
             pltpu.VMEM((256, 512), BF16),
             pltpu.VMEM((256, 512), BF16),
             pltpu.VMEM((16, 4, 2, 64, 128), F32),
@@ -269,6 +280,7 @@
             pltpu.VMEM((16, 2, 4, 4, 2, 8, 128), F32),
             pltpu.VMEM((16, 2, 4, 4, 2, 8, 128), F32),
             dma((4, 4)),
+            dma((2,)),
             dma((16,)),
             dma((16,)),
             dma((16,)),
@@ -277,16 +289,17 @@
             dma((16,)),
         ],
         compiler_params=pltpu.CompilerParams(
-            collective_id=0, has_side_effects=True, vmem_limit_bytes=48 * 2**20
+            collective_id=0, has_side_effects=True, vmem_limit_bytes=54 * 2**20
         ),
         name="exchange",
     )(species, table)
 
 
-def mix_kernel(modes_ref, coupling_ref, symbol_x_ref, symbol_y_ref, symbol_z_ref, out_ref):
-    block = out_ref.shape[1]
-    first = pl.program_id(0) * block
-    first_x = lax.axis_index("py") * 128 + first
+def mix_kernel(
+    modes_ref, coupling_ref, symbol_x_ref, symbol_y_ref, symbol_z_ref, out_ref, mixed, out_sem
+):
+    block = 128 // MIX_STEPS
+    first_x = lax.axis_index("py") * 128
     first_y = lax.axis_index("pz") * 8
     row_y = lax.broadcasted_iota(jnp.int32, (8, 256), 0)
     symbol_yz = 1.0 + jnp.broadcast_to(symbol_z_ref[...], (8, 256))
@@ -295,25 +308,33 @@
         part_y = jnp.where(row_y == k, symbol_y_ref[first_y + k], part_y)
     symbol_yz = symbol_yz + part_y
 
-    for row in range(block):
-        for part in range(2):
-            lanes = slice(128 * part, 128 * part + 128)
-            weight = 1.0 / (symbol_x_ref[first_x + row] + symbol_yz[:, lanes])
-            old = [modes_ref[a, part, first + row] for a in range(4)]
-            for a in range(4):
-                mixed = coupling_ref[a, 0] * old[0]
-                for b in range(1, 4):
-                    mixed += coupling_ref[a, b] * old[b]
-                out_ref[a, row, :, lanes] = mixed + weight * (old[a] - mixed)
+    def store(step):
+        rows = pl.ds(block * step, block)
+        return pltpu.make_async_copy(mixed.at[:, rows], out_ref.at[:, rows], out_sem.at[step])
+
+    @pl.loop(0, MIX_STEPS)
+    def _(step):
+        for k in range(block):
+            row = block * step + k
+            for part in range(2):
+                lanes = slice(128 * part, 128 * part + 128)
+                weight = 1.0 / (symbol_x_ref[first_x + row] + symbol_yz[:, lanes])
+                old = [modes_ref[a, part, row] for a in range(4)]
+                for a in range(4):
+                    total = coupling_ref[a, 0] * old[0]
+                    for b in range(1, 4):
+                        total += coupling_ref[a, b] * old[b]
+                    mixed[a, row, :, lanes] = total + weight * (old[a] - total)
+        store(step).start()
+
+    for step in range(MIX_STEPS):
+        store(step).wait()
 
 
 def mix(modes, coupling, symbol_x, symbol_y, symbol_z):
-    steps = 8
-    block = 128 // steps
     smem = pl.BlockSpec(memory_space=pltpu.SMEM)
     return pl.pallas_call(
         mix_kernel,
-        grid=(steps,),
         out_shape=jax.ShapeDtypeStruct((4, 128, 8, 256), F32),
         in_specs=[
             pl.BlockSpec(memory_space=pltpu.VMEM),
@@ -322,7 +343,11 @@
             smem,
             pl.BlockSpec(memory_space=pltpu.VMEM),
         ],
-        out_specs=pl.BlockSpec((4, block, 8, 256), lambda i: (0, i, 0, 0)),
+        out_specs=pl.BlockSpec(memory_space=pl.ANY),
+        scratch_shapes=[
+            pltpu.VMEM((4, 128, 8, 256), F32),
+            pltpu.SemaphoreType.DMA((MIX_STEPS,)),
+        ],
         compiler_params=pltpu.CompilerParams(vmem_limit_bytes=12 * 2**20),
         name="mix",
     )(modes, coupling, symbol_x, symbol_y, symbol_z.reshape(1, 256))

time: 73.1 us -> 70.3 us (0.962)
  Pallas kernels: 71.5 us -> 70.1 us
  local copies, waits for them, and re-layouts: 1.42 us -> 0.02 us
    unnamed x10 -> x8, local copies, waits for them, and re-layouts: 1.42 us -> 0.02 us
    pallas_call x2, Pallas kernels: 71.5 us -> 70.1 us  [the longest x1 67 us: exchange(): pl.pallas_call(exchange_kernel, out_shape=pltpu.VMEM((4, 2, 128, 8, 128),...]
where the time goes in v2:
time: 70.3 us; the launch traced here: 70.2 us
  Pallas kernels  70.1 us (100%)
    pallas_call x1, Pallas kernels, exchange(): pl.pallas_call(exchange_kernel, out_shape=pltpu.VMEM((4, 2, 128, 8, 128),...  67 us
    pallas_call x1, Pallas kernels, mix(): pl.pallas_call(mix_kernel, out_shape=jax.ShapeDtypeStruct((4, 128, 8, 256...  3.1 us

profile of v2, /device:TPU:1, one launch (start us, length us, event | category | flops | bytes accessed | tf_op | source)
XLA Modules:
  0.0 70.2 jit_solution(13526034425169174550)
XLA Ops:
  0.0 0.0 copy-start
  0.0 0.0 copy-start.1
  0.0 0.0 copy-start.2
  0.0 0.0 copy-start.3
  0.0 67.0 %exchange.1.modes_ref = f32[4,2,128,8,128]{4,3,2,1,0:T(8,128)S(1)} custom-call(f32[4,64,8,512]{3,2,1,0:T(8,128)} %bitcast.3, bf16[1536,512]{1,0:T(8,128)(2,1)} %constant.2.clone.table_hbm), custom_call_target="tpu_custom_call" | custom-call | tf_op jit(solution)/shard_map/exchange/pallas_call | solution.py:264
  67.0 0.0 copy-done
  67.0 0.0 copy-done.1
  67.1 0.0 copy-done.2
  67.1 0.0 copy-done.3
  67.1 3.1 %mix.1 = f32[4,128,8,256]{3,2,1,0:T(8,128)} custom-call(f32[4,2,128,8,128]{4,3,2,1,0:T(8,128)S(1)} %exchange.1.modes_ref, f32[4,4]{1,0:T(4,128)S(1)} %copy-done, f32[512]{0:T(512)S(1)} %copy-done.1, f32[256]{0:T(256)S(1)} %copy-done.2, f32[1,256]{1,0:T(1,128)S(1)} %bitcast.2), custom_call_target="tpu_custom_call" | custom-call | tf_op jit(solution)/shard_map/mix/pallas_call | solution.py:336
Async XLA Ops:
  0.0 67.0 %copy-start = (f32[4,4]{1,0:T(4,128)S(1)}, f32[4,4]{1,0:T(4,128)}, u32[]{:S(2)}) copy-start(f32[4,4]{1,0:T(4,128)} %coupling_ref.1) | copy-start | bytes 196
  0.0 67.0 %copy-start.1 = (f32[512]{0:T(512)S(1)}, f32[512]{0:T(512)}, u32[]{:S(2)}) copy-start(f32[512]{0:T(512)} %symbol_x_ref.1) | copy-start | bytes 6148
  0.0 67.1 %copy-start.2 = (f32[256]{0:T(256)S(1)}, f32[256]{0:T(256)}, u32[]{:S(2)}) copy-start(f32[256]{0:T(256)} %symbol_y_ref.1) | copy-start | bytes 3076
  0.0 67.1 %copy-start.3 = (f32[256]{0:T(256)S(1)}, f32[256]{0:T(256)}, u32[]{:S(2)}) copy-start(f32[256]{0:T(256)} %param.10) | copy-start | bytes 3076

commit v3 on v2

--- a/solution.py
+++ b/solution.py
@@ -39,9 +39,10 @@
 
 
 def exchange_kernel(
-    species_ref, table_hbm, modes_ref,
-    xin, table, lhs_high, lhs_low, ysend, yrecv, p1send, p1recv, final,
-    in_sem, table_sem, ys_sem, yr_sem, p1s_sem, p1r_sem, p2s_sem, p2r_sem,
+    species_ref, table_hbm, coupling_hbm, symbol_x_hbm, symbol_y_hbm, symbol_z_hbm,
+    modes_ref, weight_ref, coupling_ref,
+    coupling, symbol_x, symbol_y, symbol_z, xin, table, lhs_high, lhs_low, ysend, yrecv, p1send, p1recv, final,
+    in_sem, table_sem, small_sem, ys_sem, yr_sem, p1s_sem, p1r_sem, p2s_sem, p2r_sem,
 ):
     me_y = lax.axis_index("py")
     me_pz = lax.axis_index("pz")
@@ -89,6 +90,27 @@
         for copy in load_field(field):
             copy.start()
     tables[1].start()
+    smalls = [
+        pltpu.make_async_copy(coupling_hbm, coupling, small_sem.at[0]),
+        pltpu.make_async_copy(symbol_x_hbm, symbol_x, small_sem.at[1]),
+        pltpu.make_async_copy(symbol_y_hbm, symbol_y, small_sem.at[2]),
+        pltpu.make_async_copy(symbol_z_hbm, symbol_z, small_sem.at[3]),
+    ]
+    for copy in smalls:
+        copy.start()
+
+    def weights(step):
+        row_y = lax.broadcasted_iota(jnp.int32, (8, 128), 0)
+        for part in range(2):
+            lanes = pl.ds(128 * part, 128)
+            symbol_yz = 1.0 + jnp.broadcast_to(symbol_z[:, lanes], (8, 128))
+            part_y = jnp.zeros((8, 128), F32)
+            for k in range(8):
+                part_y = jnp.where(row_y == k, symbol_y[me_pz * 8 + k], part_y)
+            symbol_yz = symbol_yz + part_y
+            for k in range(16):
+                row = 16 * step + k
+                weight_ref[part, row] = 1.0 / (symbol_x[me_y * 128 + row] + symbol_yz)
 
     def x_stage(field, half):
         for plane in range(4):
@@ -111,7 +133,7 @@
                     ] = out[64 * plane : 64 * plane + 64, 128 * part : 128 * part + 128]
 
     def y_send(piece):
-        for d in (1, 3, 2):
+        for d in (2, 1, 3):
             to = lax.rem(me_y + d, 4)
             pltpu.make_async_remote_copy(
                 src_ref=ysend.at[piece, to],
@@ -137,7 +159,7 @@
             )
 
     def first_send(piece):
-        for d in (1, 3, 2):
+        for d in (2, 1, 3):
             for plane in range(2):
                 if plane == 0:
                     to = lax.rem(me_x + d, 4)
@@ -159,7 +181,7 @@
         for plane in range(2):
             arrived = p1recv.at[piece, plane, pl.ds(0, 3)]
             pltpu.make_async_copy(arrived, arrived, p1r_sem.at[piece, plane]).wait()
-            for d in (1, 3, 2, 0):
+            for d in (2, 1, 3, 0):
                 for c in (me_c, 1 - me_c):
                     if d == 0 and c is me_c:
                         continue
@@ -214,6 +236,11 @@
         y_send(2 * group + 1)
 
     tables[1].wait()
+    for copy in smalls:
+        copy.wait()
+    for a in range(4):
+        for b in range(4):
+            coupling_ref[4 * a + b] = jnp.full((8, 128), coupling[a, b], F32)
 
     @pl.loop(0, 8)
     def _(step):
@@ -239,6 +266,8 @@
             @pl.when(piece >= LAG)
             def _():
                 second_send(piece - LAG)
+
+        weights(step)
 
         @pl.when((step == 4) | (step == 6))
         def _():
@@ -259,17 +288,22 @@
         pltpu.make_async_copy(sent, sent, p2s_sem.at[piece]).wait()
 
 
-def exchange(species, table):
+def exchange(species, table, coupling, symbol_x, symbol_y, symbol_z):
     dma = pltpu.SemaphoreType.DMA
     return pl.pallas_call(
         exchange_kernel,
-        out_shape=pltpu.VMEM((4, 2, 128, 8, 128), F32),
-        in_specs=[
-            pl.BlockSpec(memory_space=pl.ANY),
-            pl.BlockSpec(memory_space=pl.ANY),
-        ],
-        out_specs=pl.BlockSpec(memory_space=pltpu.VMEM),
+        out_shape=(
+            pltpu.VMEM((4, 2, 128, 8, 128), F32),
+            pltpu.VMEM((2, 128, 8, 128), F32),
+            pltpu.VMEM((16, 8, 128), F32),
+        ),
+        in_specs=[pl.BlockSpec(memory_space=pl.ANY)] * 6,
+        out_specs=[pl.BlockSpec(memory_space=pltpu.VMEM)] * 3,
         scratch_shapes=[
+            pltpu.SMEM((4, 4), F32),
+            pltpu.SMEM((512,), F32),
+            pltpu.SMEM((256,), F32),
+            pltpu.VMEM((1, 256), F32),
             pltpu.VMEM((4, 4, 64, 8, 128), F32),
             pltpu.VMEM((1536, 512), BF16),
             pltpu.VMEM((256, 512), BF16),
@@ -281,6 +315,7 @@
             pltpu.VMEM((16, 2, 4, 4, 2, 8, 128), F32),
             dma((4, 4)),
             dma((2,)),
+            dma((4,)),
             dma((16,)),
             dma((16,)),
             dma((16,)),
@@ -292,21 +327,11 @@
             collective_id=0, has_side_effects=True, vmem_limit_bytes=54 * 2**20
         ),
         name="exchange",
-    )(species, table)
-
-
-def mix_kernel(
-    modes_ref, coupling_ref, symbol_x_ref, symbol_y_ref, symbol_z_ref, out_ref, mixed, out_sem
-):
+    )(species, table, coupling, symbol_x, symbol_y, symbol_z.reshape(1, 256))
+
+
+def mix_kernel(modes_ref, weight_ref, coupling_ref, out_ref, mixed, out_sem):
     block = 128 // MIX_STEPS
-    first_x = lax.axis_index("py") * 128
-    first_y = lax.axis_index("pz") * 8
-    row_y = lax.broadcasted_iota(jnp.int32, (8, 256), 0)
-    symbol_yz = 1.0 + jnp.broadcast_to(symbol_z_ref[...], (8, 256))
-    part_y = jnp.zeros((8, 256), F32)
-    for k in range(8):
-        part_y = jnp.where(row_y == k, symbol_y_ref[first_y + k], part_y)
-    symbol_yz = symbol_yz + part_y
 
     def store(step):
         rows = pl.ds(block * step, block)
@@ -318,12 +343,12 @@
             row = block * step + k
             for part in range(2):
                 lanes = slice(128 * part, 128 * part + 128)
-                weight = 1.0 / (symbol_x_ref[first_x + row] + symbol_yz[:, lanes])
+                weight = weight_ref[part, row]
                 old = [modes_ref[a, part, row] for a in range(4)]
                 for a in range(4):
-                    total = coupling_ref[a, 0] * old[0]
+                    total = coupling_ref[4 * a] * old[0]
                     for b in range(1, 4):
-                        total += coupling_ref[a, b] * old[b]
+                        total += coupling_ref[4 * a + b] * old[b]
                     mixed[a, row, :, lanes] = total + weight * (old[a] - total)
         store(step).start()
 
@@ -331,18 +356,11 @@
         store(step).wait()
 
 
-def mix(modes, coupling, symbol_x, symbol_y, symbol_z):
-    smem = pl.BlockSpec(memory_space=pltpu.SMEM)
+def mix(modes, weight, coupling):
     return pl.pallas_call(
         mix_kernel,
         out_shape=jax.ShapeDtypeStruct((4, 128, 8, 256), F32),
-        in_specs=[
-            pl.BlockSpec(memory_space=pltpu.VMEM),
-            smem,
-            smem,
-            smem,
-            pl.BlockSpec(memory_space=pltpu.VMEM),
-        ],
+        in_specs=[pl.BlockSpec(memory_space=pltpu.VMEM)] * 3,
         out_specs=pl.BlockSpec(memory_space=pl.ANY),
         scratch_shapes=[
             pltpu.VMEM((4, 128, 8, 256), F32),
@@ -350,15 +368,17 @@
         ],
         compiler_params=pltpu.CompilerParams(vmem_limit_bytes=12 * 2**20),
         name="mix",
-    )(modes, coupling, symbol_x, symbol_y, symbol_z.reshape(1, 256))
+    )(modes, weight, coupling)
 
 
 def shards(species, coupling, symbol_x, symbol_y, symbol_z):
     table_z = mode_table(256).reshape(32, 8, 256).transpose(1, 0, 2).reshape(256, 256)
     tables_yz = np.concatenate([halves(mode_table(256)), halves(table_z)], axis=1)
     table = np.concatenate([halves(mode_table(512)), tables_yz], axis=0)
-    modes = exchange(species.transpose(0, 2, 3, 1), table)
-    return mix(modes, coupling, symbol_x, symbol_y, symbol_z)
+    modes, weight, splats = exchange(
+        species.transpose(0, 2, 3, 1), table, coupling, symbol_x, symbol_y, symbol_z
+    )
+    return mix(modes, weight, splats)
 
 
 def solution(mesh):

time: 70.3 us -> 68.8 us (0.979)
  Pallas kernels: 70.1 us -> 68.7 us
    pallas_call x1, Pallas kernels: 3.1 us -> 2.27 us  [mix(): pl.pallas_call(mix_kernel, out_shape=jax.ShapeDtypeStruct((4, 128, 8, 256...]
where the time goes in v3:
time: 68.8 us; the launch traced here: 68.7 us
  Pallas kernels  68.7 us (100%)
    pallas_call x1, Pallas kernels, exchange(): pl.pallas_call(exchange_kernel, out_shape=(pltpu.VMEM((4, 2, 128, 8, 128)...  66.4 us
    pallas_call x1, Pallas kernels, mix(): pl.pallas_call(mix_kernel, out_shape=jax.ShapeDtypeStruct((4, 128, 8, 256...  2.27 us

profile of v3, /device:TPU:1, one launch (start us, length us, event | category | flops | bytes accessed | tf_op | source)
XLA Modules:
  0.0 68.7 jit_solution(6115309809703358863)
XLA Ops:
  0.0 66.4 %exchange.1 = (f32[4,2,128,8,128]{4,3,2,1,0:T(8,128)S(1)}, f32[2,128,8,128]{3,2,1,0:T(8,128)S(1)}, f32[16,8,128]{2,1,0:T(8,128)S(1)}) custom-call(f32[4,64,8,512]{3,2,1,0:T(8,128)} %bitcast.2, bf16[1536,512]{1,0:T(8,128)(2,1)} %constant.2.clone.table_hbm, f32[4,4]{1,0:T(4,128)} %coupling_hbm.1, f32[512]{0:T(512)} %symbol_x_hbm.1, f32[256]{0:T(256)} %symbol_y_hbm.1, ...), custom_call_target="tpu_custom_call" | custom-call | tf_op jit(solution)/shard_map/exchange/pallas_call | solution.py:293
  66.4 2.3 %mix.1 = f32[4,128,8,256]{3,2,1,0:T(8,128)} custom-call(f32[4,2,128,8,128]{4,3,2,1,0:T(8,128)S(1)} %get-tuple-element.8.modes_ref, f32[2,128,8,128]{3,2,1,0:T(8,128)S(1)} %get-tuple-element.9.weight_ref, f32[16,8,128]{2,1,0:T(8,128)S(1)} %get-tuple-element.10.coupling_ref), custom_call_target="tpu_custom_call" | custom-call | tf_op jit(solution)/shard_map/mix/pallas_call | solution.py:360
